TPU v7x, 32 devices: a whole 2x2x4 slice. The times are simulated.
32 devices in a mesh: groups: 2 (over y), fft: 4 (over z), band: 2 (over x), sub: 2 (over core).
Axes of the slice: x: 2, y: 2, z: 4, core: 2. Of those that a mesh axis runs over, the one named last changes fastest.
Arguments:
- coefficients: bfloat16 [8, 2, 128, 1024], P(('groups', 'band', 'sub'), None, None, 'fft'), parts along dimension 0, may hold values from -6 to 6
- potential: float32 [384, 192, 192], P(('groups', 'fft')), parts along dimension 0, may hold values from -15 to 15
- stick_map: int32 [3, 2048], P(None, ('groups', 'fft')), parts along dimension 1, may hold values from 0 to 191, as said below
- plane_order: int32 [384], P('groups'), parts along dimension 0, may hold values from 0 to 191, each once
Outputs:
- applied: float32 [8, 2, 128, 1024], P(('groups', 'band', 'sub'), None, None, 'fft'), parts along dimension 0
There are 2 independent parts, one for each index of `groups`. A program takes and returns all parts, laid end to end along the dimension named above; each array names one. Nothing has to cross between parts.
Inputs may be any that keep to these rules, and one draw needn't show every extreme that they name: Column s is one stick slot: stick_map[0, s] and stick_map[1, s] are its grid indices x and y, stick_map[2, s] its length, an odd number up to 127, or 0 for an empty slot. A stick of length L holds the frequencies -(L - 1)/2 to (L - 1)/2 at entries 128/2 + f. The number of live slots differs between indices of fft; some index has all 256 slots live, and 512 slots are live in all. Live sticks name distinct columns, whose frequencies (indices taken modulo 192 into -96 to 95) lie in -48 to 47 along x and along y; an empty slot may name any column. `plane_order`: each plane number appears once.
All inputs are finite; a program needn't handle non-finite values.
Results may differ from a plain program's by a relative error of at most 0.0084.
Values may be sent and summed in bfloat16 or wider, within the bound.
No kernel may reach another device: no remote copies, remote signals or barrier semaphores. Data moves between devices by JAX's collectives and lax.ppermute only.
A program may use at most 128 MiB of HBM per device.

v0:
```python
import math
import jax
import jax.numpy as jnp
from jax import lax
from jax.sharding import PartitionSpec as P


def phase_tables(left_ids, right_ids, modulus):
    turn_index = left_ids[:, None] * right_ids[None, :] % modulus
    angles = turn_index.astype(jnp.float32) * (2.0 * math.pi / modulus)
    return (jnp.cos(angles).astype(jnp.bfloat16), jnp.sin(angles).astype(jnp.bfloat16))


def row_numbers(grid_side):
    compact = jnp.arange(grid_side // 2, dtype=jnp.int32)
    return jnp.where(compact < grid_side // 4, compact, compact + grid_side // 2)


def compact_rows(grid_ids, grid_side):
    rows = jnp.where(grid_ids < grid_side // 4, grid_ids, grid_ids - grid_side // 2)
    return jnp.clip(rows, 0, grid_side // 2 - 1)


def one_hot_rows(grid_ids, grid_side):
    rows = compact_rows(grid_ids, grid_side)
    slots = jnp.arange(grid_side // 2, dtype=jnp.int32)
    return (rows[:, None] == slots[None, :]).astype(jnp.bfloat16)


def plane_work(received, x_onehot, y_onehot, sources, depth_count, grid_side, potential_rows):
    planes = received.shape[0]
    half_side = grid_side // 2
    slot_count = x_onehot.shape[0] // sources

    def place_one(row):
        values = row.reshape(sources, depth_count, 2, slot_count).transpose(1, 2, 0, 3)
        values = values.reshape(depth_count, 2, sources * slot_count)
        weighted = values[..., None] * y_onehot[None, None]
        return jnp.einsum(
            "sx,dcsy->dxcy", x_onehot, weighted, preferred_element_type=jnp.float32
        ).astype(jnp.bfloat16)

    spread = lax.map(place_one, received)
    axis_ids = jnp.arange(grid_side, dtype=jnp.int32)
    live_ids = row_numbers(grid_side)
    cos_w, sin_w = phase_tables(live_ids, axis_ids, grid_side)
    forward_y = jnp.concatenate(
        [jnp.concatenate([cos_w, sin_w], 1), jnp.concatenate([-sin_w, cos_w], 1)], 0
    )
    inverse_y = jnp.concatenate(
        [jnp.concatenate([cos_w.T, -sin_w.T], 1), jnp.concatenate([sin_w.T, cos_w.T], 1)], 0
    )
    cos_x = cos_w.T
    sin_x = sin_w.T
    forward_x = jnp.concatenate([cos_x, sin_x], 0)
    inverse_x = jnp.concatenate([cos_w, sin_w], 0)
    half_y = jnp.dot(
        spread.reshape(-1, 2 * half_side), forward_y, preferred_element_type=jnp.float32
    )
    half_y = half_y.astype(jnp.bfloat16).reshape(planes, depth_count, half_side, 2 * grid_side)
    mixed_x = jnp.einsum("ux,pbxw->pbuw", forward_x, half_y, preferred_element_type=jnp.float32)
    cos_part = mixed_x[:, :, :grid_side]
    sin_part = mixed_x[:, :, grid_side:]
    pot_field = potential_rows[:, None, :, :]
    real_part = (cos_part[..., :grid_side] - sin_part[..., grid_side:]) * pot_field
    imag_part = (cos_part[..., grid_side:] + sin_part[..., :grid_side]) * pot_field
    product = jnp.concatenate([real_part, imag_part], 3).astype(jnp.bfloat16)
    mixed_x = jnp.einsum("ux,pbxw->pbuw", inverse_x, product, preferred_element_type=jnp.float32)
    cos_part = mixed_x[:, :, :half_side]
    sin_part = mixed_x[:, :, half_side:]
    back_x = jnp.concatenate(
        [
            cos_part[..., :grid_side] + sin_part[..., grid_side:],
            cos_part[..., grid_side:] - sin_part[..., :grid_side],
        ],
        3,
    ).astype(jnp.bfloat16)
    back_y = jnp.dot(
        back_x.reshape(-1, 2 * grid_side), inverse_y, preferred_element_type=jnp.float32
    ).astype(jnp.bfloat16)
    back_y = back_y.reshape(planes, depth_count, half_side, 2, half_side)

    def pick_one(grid):
        picked = jnp.einsum("sx,dxcy->dcsy", x_onehot, grid, preferred_element_type=jnp.float32)
        values = jnp.sum(picked * y_onehot[None, None], axis=3)
        values = values.reshape(depth_count, 2, sources, slot_count).transpose(2, 0, 1, 3)
        return values.reshape(-1).astype(jnp.bfloat16)

    return lax.map(pick_one, back_y)


def body(coefficients, potential, stick_map, plane_order):
    band_count = coefficients.shape[0]
    z_span = coefficients.shape[2]
    slot_count = coefficients.shape[3]
    grid_side = potential.shape[1]
    entries = jnp.arange(z_span, dtype=jnp.int32)
    freq_z = (entries - z_span // 2) % grid_side
    half_len = (stick_map[2] - 1) // 2
    keep_mask = jnp.abs(entries[:, None] - z_span // 2) <= half_len[None, :]
    masked = coefficients * keep_mask.astype(jnp.bfloat16)
    cos_z, sin_z = phase_tables(plane_order, freq_z, grid_side)
    forward_z = jnp.stack(
        [jnp.concatenate([cos_z, -sin_z], 1), jnp.concatenate([sin_z, cos_z], 1)], 1
    )
    sticks = jnp.einsum(
        "zck,bks->zbcs",
        forward_z,
        masked.reshape(band_count, 2 * z_span, slot_count),
        preferred_element_type=jnp.float32,
    )
    sticks = sticks.astype(jnp.bfloat16).reshape(grid_side, band_count * 2 * slot_count)
    columns = lax.all_gather(stick_map, "fft", axis=1, tiled=True)
    sources = lax.axis_size("fft")
    x_onehot = one_hot_rows(columns[0], grid_side)
    y_onehot = one_hot_rows(columns[1], grid_side)
    copies = lax.axis_size("sub")
    plane_share = potential.shape[0] // copies
    potential_rows = lax.dynamic_slice_in_dim(
        potential, lax.axis_index("sub") * plane_share, plane_share, 0
    )
    received = lax.all_to_all(sticks, ("fft", "sub"), split_axis=0, concat_axis=1, tiled=True)
    gathered = plane_work(
        received, x_onehot, y_onehot, sources, copies * band_count, grid_side, potential_rows
    )
    returned = lax.all_to_all(gathered, ("fft", "sub"), split_axis=1, concat_axis=0, tiled=True)
    inverse_z = jnp.stack([jnp.stack([cos_z, sin_z], 1), jnp.stack([-sin_z, cos_z], 1)], 1)
    totals = jnp.einsum(
        "rcdk,rbds->bcks",
        inverse_z,
        returned.reshape(grid_side, band_count, 2, slot_count),
        preferred_element_type=jnp.float32,
    )
    return totals * (keep_mask.astype(jnp.float32) * (1.0 / grid_side**3))


def solution(mesh):
    placed = (
        P(("groups", "band", "sub"), None, None, "fft"),
        P(("groups", "fft"), None, None),
        P(None, ("groups", "fft")),
        P("groups"),
    )
    return jax.shard_map(
        body,
        mesh=mesh,
        in_specs=placed,
        out_specs=P(("groups", "band", "sub"), None, None, "fft"),
        check_vma=False,
    )
```

profile of v0, /device:TPU:0, one launch (start us, length us, event | category | flops | bytes accessed | tf_op | source)
XLA Modules:
  0.0 154.8 jit_solution(12331591917178488166)
XLA Ops:
  0.0 1.2 sine_convert_fusion.3
  1.2 1.1 fusion.86
  2.3 0.7 and_select_fusion
  3.3 0.9 broadcast_multiply_fusion
  4.6 0.8 all_to_all.26
  5.4 6.4 %all-to-all-start = ((bf16[8,24,512]{2,1,0:T(8,128)(2,1)}), bf16[8,24,512]{2,1,0:T(8,128)(2,1)S(1)}, u32[]{:S(2)}, u32[]{:S(2)}) async-start(bf16[8,24,512]{2,1,0:T(8,128)(2,1)} %all_to_all.26), calls=%async_computation | async-start | bytes 393216 | tf_op jit(solution)/shard_map/all_to_all | solution.py:122
  11.8 15.4 %all_gather.3 = s32[3,1024]{1,0:T(4,128)S(1)} all-gather(s32[3,256]{1,0:T(4,128)} %param.10), channel_id=1, replica_groups=mesh['groups'=2,'fft'=4,'band'=2,'sub'=2] {'fft'}, dimensions={1}, use_global_device_ids=true | all-gather | bytes 15360 | tf_op jit(solution)/shard_map/all_gather | solution.py:113
  27.2 0.5 sine_convert_fusion.2
  27.7 0.5 fusion.84
  28.2 0.5 cosine_convert_fusion.1
  28.7 0.5 fusion.85
  29.2 1.2 sine_convert_fusion
  30.3 1.1 fusion.87
  31.5 4.9 %constant_dynamic-slice_fusion.1 = f32[24,192,192]{2,1,0:T(8,128)} fusion(f32[48,192,192]{2,1,0:T(8,128)} %param.9, s32[]{:T(128)S(6)} %select_n.131), kind=kLoop, calls=%fused_computation.140 | loop fusion | bytes 7077892 | tf_op jit(solution)/shard_map/dynamic_slice | solution.py:119
  36.4 30.9 %while.22 = (s32[]{:T(128)}, bf16[24,2,96,2,96]{2,1,0,4,3:T(2,128)(2,1)}, bf16[24,4096]{1,0:T(8,128)(2,1)S(1)}, s32[1024]{0:T(1024)S(1)}, s32[1024]{0:T(1024)S(1)}, /*index=5*/s32[]{:T(128)}) while((s32[]{:T(128)}, bf16[24,2,96,2,96]{2,1,0,4,3:T(2,128)(2,1)}, bf16[24,4096]{1,0:T(8,128)(2,1)S(1)}, s32[1024]{0:T(1024)S(1)}, ...), condition=%wide.region_1.2_spmd.clone, body=%wide.region_0.1_spmd.clone.sunk | while | flops 76320768 | bytes 705097 | solution.py:43
  37.1 0.8 copy_dynamic-update-slice_fusion.2
  38.4 0.8 copy_dynamic-update-slice_fusion.2
  39.7 0.8 copy_dynamic-update-slice_fusion.2
  41.0 0.8 copy_dynamic-update-slice_fusion.2
  42.3 0.8 copy_dynamic-update-slice_fusion.2
  43.6 0.8 copy_dynamic-update-slice_fusion.2
  44.8 0.8 copy_dynamic-update-slice_fusion.2
  46.1 0.8 copy_dynamic-update-slice_fusion.2
  47.4 0.8 copy_dynamic-update-slice_fusion.2
  48.6 0.8 copy_dynamic-update-slice_fusion.2
  49.9 0.8 copy_dynamic-update-slice_fusion.2
  51.2 0.7 copy_dynamic-update-slice_fusion.2
  52.5 0.8 copy_dynamic-update-slice_fusion.2
  53.8 0.8 copy_dynamic-update-slice_fusion.2
  55.1 0.8 copy_dynamic-update-slice_fusion.2
  56.3 0.8 copy_dynamic-update-slice_fusion.2
  57.6 0.8 copy_dynamic-update-slice_fusion.2
  58.9 0.8 copy_dynamic-update-slice_fusion.2
  60.2 0.8 copy_dynamic-update-slice_fusion.2
  61.5 0.8 copy_dynamic-update-slice_fusion.2
  62.7 0.8 copy_dynamic-update-slice_fusion.2
  64.0 0.8 copy_dynamic-update-slice_fusion.2
  65.3 0.8 copy_dynamic-update-slice_fusion.2
  66.6 0.8 copy_dynamic-update-slice_fusion.2
  67.4 7.0 %reshape.324 = bf16[4608,192]{0,1:T(8,128)(2,1)S(1)} reshape(bf16[24,2,96,2,96]{2,1,0,4,3:T(2,128)(2,1)} %get-tuple-element.59) | data formatting | bytes 3538944 | tf_op jit(solution)/shard_map/reshape | solution.py:58
  74.4 1.5 convolution_convert_fusion.1
  75.9 11.5 %convolution_bitcast_fusion = f32[24,2,384,384]{3,2,1,0:T(8,128)} fusion(bf16[24,2,96,384]{3,2,1,0:T(8,128)(2,1)S(1)} %bitcast.104, bf16[192,96]{0,1:T(8,128)(2,1)S(1)} %get-tuple-element.141, bf16[192,96]{0,1:T(8,128)(2,1)S(1)} %get-tuple-element.140), kind=kOutput, calls=%fused_computation.28 | convolution fusion | flops 1359101952 | bytes 31924224 | tf_op jit(solution)/shard_map/ux,pbxw->pbuw/dot_general | solution.py:61
  87.3 16.3 %fusion.27 = (bf16[24,2,192,192]{3,2,1,0:T(8,128)(2,1)S(1)}, bf16[24,2,192,192]{3,2,1,0:T(8,128)(2,1)}) fusion(f32[24,2,384,384]{3,2,1,0:T(8,128)} %convolution_bitcast_fusion, f32[24,192,192]{2,1,0:T(8,128)S(1)} %bitcast.106), kind=kLoop, calls=%fused_computation.34 | loop fusion | flops 10616832 | bytes 38928384 | tf_op jit(solution)/shard_map/convert.4
  103.6 4.9 %convolution_bitcast_fusion.1 = f32[24,2,192,384]{3,2,1,0:T(8,128)S(1)} fusion(bf16[24,2,192,192]{3,2,1,0:T(8,128)(2,1)} %get-tuple-element.127, bf16[24,2,192,192]{3,2,1,0:T(8,128)(2,1)S(1)} %get-tuple-element.126, bf16[96,192]{1,0:T(8,128)(2,1)S(1)} %get-tuple-element.142, bf16[96,192]{1,0:T(8,128)(2,1)S(1)} %get-tuple-element.143), kind=kOutput, calls=%fused_computation.35 | convolution fusion | flops 1373257728 | bytes 21307392 | tf_op jit(solution)/shard_map/ux,pbxw->pbuw/dot_general | solution.py:68
  108.5 3.1 %fusion.32 = (bf16[24,2,96,192]{3,2,1,0:T(8,128)(2,1)S(1)}, bf16[24,2,96,192]{3,2,1,0:T(8,128)(2,1)S(1)}) fusion(f32[24,2,192,384]{3,2,1,0:T(8,128)S(1)} %convolution_bitcast_fusion.1), kind=kLoop, calls=%fused_computation.44 | loop fusion | flops 3538944 | bytes 17694720 | tf_op jit(solution)/shard_map/convert.3
  111.5 2.8 %convolution_convert_fusion.2 = bf16[4608,192]{0,1:T(8,128)(2,1)} fusion(bf16[4608,192]{1,0:T(8,128)(2,1)S(1)} %bitcast.108, bf16[4608,192]{1,0:T(8,128)(2,1)S(1)} %bitcast.107, bf16[192,96]{0,1:T(8,128)(2,1)S(1)} %get-tuple-element.140, bf16[192,96]{0,1:T(8,128)(2,1)S(1)} %get-tuple-element.141, bf16[192,96]{0,1:T(8,128)(2,1)S(1)} %fusion.85), kind=kOutput, calls=%fused_computation.40 | convolution fusion | flops 688029696 | bytes 5419008 | tf_op jit(solution)/shard_map/dot_general | solution.py:78
  114.3 7.7 %reshape.326 = bf16[24,2,96,2,96]{2,1,0,4,3:T(2,128)(2,1)S(1)} reshape(bf16[4608,192]{0,1:T(8,128)(2,1)} %convolution_convert_fusion.2) | data formatting | bytes 3538944 | tf_op jit(solution)/shard_map/reshape | solution.py:81
  122.0 19.3 %while.23 = (s32[]{:T(128)}, bf16[24,4096]{1,0:T(8,128)(2,1)S(1)}, bf16[24,2,96,2,96]{2,1,0,4,3:T(2,128)(2,1)S(1)}, s32[1024]{0:T(1024)S(1)}, s32[1024]{0:T(1024)S(1)}, /*index=5*/s32[]{:T(128)}, s32[]{:T(128)}) while((s32[]{:T(128)}, bf16[24,4096]{1,0:T(8,128)(2,1)S(1)}, bf16[24,2,96,2,96]{2,1,0,4,3:T(2,128)(2,1)S(1)}, ...), condition=%wide.region_4.5_spmd.clone, body=%wide.region_2.4_spmd.clone.sunk | while | flops 76771328 | bytes 1089621 | solution.py:89
  123.7 0.4 fusion.114
  125.3 0.4 fusion.114
  126.9 0.4 fusion.114
  128.5 0.4 fusion.114
  130.2 0.4 fusion.114
  131.8 0.4 fusion.114
  133.4 0.4 fusion.114
  135.0 0.4 fusion.114
  136.6 0.4 fusion.114
  137.4 0.4 fusion.114
  138.2 0.4 fusion.114
  139.8 0.4 fusion.114
  141.3 0.7 copy.44
  142.0 3.4 %all-to-all-start.1 = ((bf16[24,8,512]{2,0,1:T(8,128)(2,1)}), bf16[24,8,512]{2,0,1:T(8,128)(2,1)S(1)}, u32[]{:S(2)}, u32[]{:S(2)}) async-start(bf16[24,8,512]{2,0,1:T(8,128)(2,1)} %bitcast.87), calls=%async_computation.1 | async-start | bytes 393216 | tf_op jit(solution)/shard_map/all_to_all | solution.py:126
  145.5 8.1 %all-to-all-done.1 = bf16[24,8,512]{2,0,1:T(8,128)(2,1)S(1)} async-done(((bf16[24,8,512]{2,0,1:T(8,128)(2,1)}), bf16[24,8,512]{2,0,1:T(8,128)(2,1)S(1)}, u32[]{:S(2)}, u32[]{:S(2)}) %all-to-all-start.1) | async-done | bytes 196640 | tf_op jit(solution)/shard_map/all_to_all | solution.py:126
  153.9 0.8 copy.24
  (299 shorter events, 26.3 us)
Async XLA Ops:
  5.4 31.0 %all-to-all-start = ((bf16[8,24,512]{2,1,0:T(8,128)(2,1)}), bf16[8,24,512]{2,1,0:T(8,128)(2,1)S(1)}, u32[]{:S(2)}, u32[]{:S(2)}) async-start(bf16[8,24,512]{2,1,0:T(8,128)(2,1)} %all_to_all.26), calls=%async_computation | async-start | bytes 393216 | tf_op jit(solution)/shard_map/all_to_all | solution.py:122
  74.3 13.0 %slice-start = ((s8[4718592]{0:T(1024)(128)(4,1)}), s8[4194304]{0:T(1024)(128)(4,1)S(1)}, s32[]{:S(2)}) async-start(s8[4718592]{0:T(1024)(128)(4,1)} %bitcast.105), calls=%async_computation.2 | async-start | bytes 8388608
  75.9 11.5 %slice-start.1 = ((s8[4718592]{0:T(1024)(128)(4,1)}), s8[524288]{0:T(1024)(128)(4,1)S(1)}, s32[]{:S(2)}) async-start(s8[4718592]{0:T(1024)(128)(4,1)} %bitcast.105), calls=%async_computation.3 | async-start | bytes 1048576
  142.0 11.6 %all-to-all-start.1 = ((bf16[24,8,512]{2,0,1:T(8,128)(2,1)}), bf16[24,8,512]{2,0,1:T(8,128)(2,1)S(1)}, u32[]{:S(2)}, u32[]{:S(2)}) async-start(bf16[24,8,512]{2,0,1:T(8,128)(2,1)} %bitcast.87), calls=%async_computation.1 | async-start | bytes 393216 | tf_op jit(solution)/shard_map/all_to_all | solution.py:126
where the time goes:
time: 155 us
  local copies, waits for them, and re-layouts  51.1 us (33%)
  matrix products  38.7 us (25%)
  other arithmetic  29.4 us (19%)
  blocking collectives  15.4 us (10%)
  starting transfers between devices  9.75 us (6%)
  waiting for transfers between devices  8.1 us (5%)
  loops' own time  2.11 us (1%)
    another operation x2, other arithmetic  19.3 us
    dynamic_update_slice x24, local copies, waits for them, and re-layouts, plane_work(): spread = lax.map(place_one, received)  18.5 us
    all_gather x1, blocking collectives, body(): columns = lax.all_gather(stick_map, 'fft', axis=1, tiled=True)  15.4 us
    dot_general x1, matrix products, plane_work(): jnp.einsum('ux,pbxw->pbuw', forward_x, half_y, preferred_element_type=jnp...  11.5 us
    dot_general x24, matrix products, pick_one(): jnp.einsum('sx,dxcy->dcsy', x_onehot, grid, preferred_element_type=jnp.fl...  8.95 us
    dot_general x24, matrix products, place_one(): jnp.einsum('sx,dcsy->dxcy', x_onehot, weighted, preferred_element_type=jn...  8.66 us
    all_to_all x1, waiting for transfers between devices, body(): lax.all_to_all(gathered, ('fft', 'sub'), split_axis=1, concat_axis=0, til...  8.1 us
    reshape x1, local copies, waits for them, and re-layouts, plane_work(): back_y = back_y.reshape(planes, depth_count, half_side, 2, half_side)  7.68 us
  transfers between devices with their start and end apart: 2, of which 1 were waited for; matrix products, arithmetic and copies ran while one was open for 6% of the time, Pallas kernels for 0%

commit v1 on v0

--- a/solution.py
+++ b/solution.py
@@ -110,7 +110,7 @@
         preferred_element_type=jnp.float32,
     )
     sticks = sticks.astype(jnp.bfloat16).reshape(grid_side, band_count * 2 * slot_count)
-    columns = lax.all_gather(stick_map, "fft", axis=1, tiled=True)
+    columns = jnp.concatenate(lax.all_gather(stick_map, "fft"), axis=1)
     sources = lax.axis_size("fft")
     x_onehot = one_hot_rows(columns[0], grid_side)
     y_onehot = one_hot_rows(columns[1], grid_side)

time: 155 us -> 155 us (level)
  no operation moved by 1% of the time
where the time goes in v1:
time: 155 us; the launch traced here: 154 us
  local copies, waits for them, and re-layouts  51.1 us (33%)
  matrix products  38.7 us (25%)
  other arithmetic  29.4 us (19%)
  blocking collectives  13.9 us (9%)
  starting transfers between devices  10.9 us (7%)
  waiting for transfers between devices  8.18 us (5%)
  loops' own time  2.11 us (1%)
    another operation x2, other arithmetic  19.3 us
    dynamic_update_slice x24, local copies, waits for them, and re-layouts, plane_work(): spread = lax.map(place_one, received)  18.5 us
    all_gather x1, blocking collectives, body(): columns = jnp.concatenate(lax.all_gather(stick_map, 'fft'), axis=1)  13.9 us
    dot_general x1, matrix products, plane_work(): jnp.einsum('ux,pbxw->pbuw', forward_x, half_y, preferred_element_type=jnp...  11.5 us
    dot_general x24, matrix products, pick_one(): jnp.einsum('sx,dxcy->dcsy', x_onehot, grid, preferred_element_type=jnp.fl...  8.95 us
    dot_general x24, matrix products, place_one(): jnp.einsum('sx,dcsy->dxcy', x_onehot, weighted, preferred_element_type=jn...  8.66 us
    all_to_all x1, waiting for transfers between devices, body(): lax.all_to_all(gathered, ('fft', 'sub'), split_axis=1, concat_axis=0, til...  8.18 us
    reshape x1, local copies, waits for them, and re-layouts, plane_work(): back_y = back_y.reshape(planes, depth_count, half_side, 2, half_side)  7.68 us
  transfers between devices with their start and end apart: 2, of which 1 were waited for; matrix products, arithmetic and copies ran while one was open for 6% of the time, Pallas kernels for 0%

profile of v1, /device:TPU:0, one launch (start us, length us, event | category | flops | bytes accessed | tf_op | source)
XLA Modules:
  0.0 154.5 jit_solution(10288718352861961293)
XLA Ops:
  0.0 1.2 sine_convert_fusion.3
  1.2 1.1 fusion.86
  2.3 0.7 and_select_fusion
  3.3 0.9 broadcast_multiply_fusion
  4.6 0.8 all_to_all.26
  5.4 6.4 %all-to-all-start = ((bf16[8,24,512]{2,1,0:T(8,128)(2,1)}), bf16[8,24,512]{2,1,0:T(8,128)(2,1)S(1)}, u32[]{:S(2)}, u32[]{:S(2)}) async-start(bf16[8,24,512]{2,1,0:T(8,128)(2,1)} %all_to_all.26), calls=%async_computation | async-start | bytes 393216 | tf_op jit(solution)/shard_map/all_to_all | solution.py:122
  11.8 0.5 sine_convert_fusion.2
  12.3 0.5 fusion.84
  12.8 0.5 cosine_convert_fusion.1
  13.3 0.5 fusion.85
  13.8 1.2 sine_convert_fusion
  14.9 1.1 fusion.87
  16.1 13.9 %all-gather.1 = s32[4,3,256]{2,1,0:T(4,128)S(1)} all-gather(s32[1,3,256]{2,1,0:T(4,128)} %bitcast.124), channel_id=2, replica_groups=mesh['groups'=2,'fft'=4,'band'=2,'sub'=2] {'fft'}, dimensions={0}, use_global_device_ids=true | all-gather | bytes 15360 | tf_op jit(solution)/shard_map/all_gather | solution.py:113
  30.0 4.9 %constant_dynamic-slice_fusion.1 = f32[24,192,192]{2,1,0:T(8,128)} fusion(f32[48,192,192]{2,1,0:T(8,128)} %param.9, s32[]{:T(128)S(6)} %select_n.131), kind=kLoop, calls=%fused_computation.140 | loop fusion | bytes 7077892 | tf_op jit(solution)/shard_map/dynamic_slice | solution.py:119
  34.9 30.9 %while.22 = (s32[]{:T(128)}, bf16[24,2,96,2,96]{2,1,0,4,3:T(2,128)(2,1)}, bf16[24,4096]{1,0:T(8,128)(2,1)S(1)}, s32[1024]{0:T(1024)S(1)}, s32[1024]{0:T(1024)S(1)}, /*index=5*/s32[]{:T(128)}) while((s32[]{:T(128)}, bf16[24,2,96,2,96]{2,1,0,4,3:T(2,128)(2,1)}, bf16[24,4096]{1,0:T(8,128)(2,1)S(1)}, s32[1024]{0:T(1024)S(1)}, ...), condition=%wide.region_1.2_spmd.clone, body=%wide.region_0.1_spmd.clone.sunk | while | flops 76320768 | bytes 705097 | solution.py:43
  35.6 0.8 copy_dynamic-update-slice_fusion.2
  36.9 0.8 copy_dynamic-update-slice_fusion.2
  38.2 0.8 copy_dynamic-update-slice_fusion.2
  39.5 0.8 copy_dynamic-update-slice_fusion.2
  40.8 0.8 copy_dynamic-update-slice_fusion.2
  42.0 0.8 copy_dynamic-update-slice_fusion.2
  43.3 0.8 copy_dynamic-update-slice_fusion.2
  44.6 0.8 copy_dynamic-update-slice_fusion.2
  45.9 0.8 copy_dynamic-update-slice_fusion.2
  47.1 0.8 copy_dynamic-update-slice_fusion.2
  48.4 0.8 copy_dynamic-update-slice_fusion.2
  49.7 0.7 copy_dynamic-update-slice_fusion.2
  51.0 0.8 copy_dynamic-update-slice_fusion.2
  52.3 0.8 copy_dynamic-update-slice_fusion.2
  53.6 0.8 copy_dynamic-update-slice_fusion.2
  54.8 0.8 copy_dynamic-update-slice_fusion.2
  56.1 0.8 copy_dynamic-update-slice_fusion.2
  57.4 0.8 copy_dynamic-update-slice_fusion.2
  58.7 0.8 copy_dynamic-update-slice_fusion.2
  60.0 0.8 copy_dynamic-update-slice_fusion.2
  61.2 0.8 copy_dynamic-update-slice_fusion.2
  62.5 0.8 copy_dynamic-update-slice_fusion.2
  63.8 0.8 copy_dynamic-update-slice_fusion.2
  65.1 0.8 copy_dynamic-update-slice_fusion.2
  65.8 7.0 %reshape.333 = bf16[4608,192]{0,1:T(8,128)(2,1)S(1)} reshape(bf16[24,2,96,2,96]{2,1,0,4,3:T(2,128)(2,1)} %get-tuple-element.59) | data formatting | bytes 3538944 | tf_op jit(solution)/shard_map/reshape | solution.py:58
  72.8 1.5 convolution_convert_fusion.1
  74.4 11.5 %convolution_bitcast_fusion = f32[24,2,384,384]{3,2,1,0:T(8,128)} fusion(bf16[24,2,96,384]{3,2,1,0:T(8,128)(2,1)S(1)} %bitcast.106, bf16[192,96]{0,1:T(8,128)(2,1)S(1)} %get-tuple-element.146, bf16[192,96]{0,1:T(8,128)(2,1)S(1)} %get-tuple-element.145), kind=kOutput, calls=%fused_computation.28 | convolution fusion | flops 1359101952 | bytes 31924224 | tf_op jit(solution)/shard_map/ux,pbxw->pbuw/dot_general | solution.py:61
  85.8 16.3 %fusion.27 = (bf16[24,2,192,192]{3,2,1,0:T(8,128)(2,1)S(1)}, bf16[24,2,192,192]{3,2,1,0:T(8,128)(2,1)}) fusion(f32[24,2,384,384]{3,2,1,0:T(8,128)} %convolution_bitcast_fusion, f32[24,192,192]{2,1,0:T(8,128)S(1)} %bitcast.108), kind=kLoop, calls=%fused_computation.34 | loop fusion | flops 10616832 | bytes 38928384 | tf_op jit(solution)/shard_map/convert.4
  102.1 4.9 %convolution_bitcast_fusion.1 = f32[24,2,192,384]{3,2,1,0:T(8,128)S(1)} fusion(bf16[24,2,192,192]{3,2,1,0:T(8,128)(2,1)} %get-tuple-element.132, bf16[24,2,192,192]{3,2,1,0:T(8,128)(2,1)S(1)} %get-tuple-element.131, bf16[96,192]{1,0:T(8,128)(2,1)S(1)} %get-tuple-element.147, bf16[96,192]{1,0:T(8,128)(2,1)S(1)} %get-tuple-element.148), kind=kOutput, calls=%fused_computation.35 | convolution fusion | flops 1373257728 | bytes 21307392 | tf_op jit(solution)/shard_map/ux,pbxw->pbuw/dot_general | solution.py:68
  107.0 3.1 %fusion.32 = (bf16[24,2,96,192]{3,2,1,0:T(8,128)(2,1)S(1)}, bf16[24,2,96,192]{3,2,1,0:T(8,128)(2,1)S(1)}) fusion(f32[24,2,192,384]{3,2,1,0:T(8,128)S(1)} %convolution_bitcast_fusion.1), kind=kLoop, calls=%fused_computation.44 | loop fusion | flops 3538944 | bytes 17694720 | tf_op jit(solution)/shard_map/convert.3
  110.0 2.8 %convolution_convert_fusion.2 = bf16[4608,192]{0,1:T(8,128)(2,1)} fusion(bf16[4608,192]{1,0:T(8,128)(2,1)S(1)} %bitcast.110, bf16[4608,192]{1,0:T(8,128)(2,1)S(1)} %bitcast.109, bf16[192,96]{0,1:T(8,128)(2,1)S(1)} %get-tuple-element.145, bf16[192,96]{0,1:T(8,128)(2,1)S(1)} %get-tuple-element.146, bf16[192,96]{0,1:T(8,128)(2,1)S(1)} %fusion.85), kind=kOutput, calls=%fused_computation.40 | convolution fusion | flops 688029696 | bytes 5419008 | tf_op jit(solution)/shard_map/dot_general | solution.py:78
  112.8 7.7 %reshape.335 = bf16[24,2,96,2,96]{2,1,0,4,3:T(2,128)(2,1)S(1)} reshape(bf16[4608,192]{0,1:T(8,128)(2,1)} %convolution_convert_fusion.2) | data formatting | bytes 3538944 | tf_op jit(solution)/shard_map/reshape | solution.py:81
  120.5 19.3 %while.23 = (s32[]{:T(128)}, bf16[24,4096]{1,0:T(8,128)(2,1)S(1)}, bf16[24,2,96,2,96]{2,1,0,4,3:T(2,128)(2,1)S(1)}, s32[1024]{0:T(1024)S(1)}, s32[1024]{0:T(1024)S(1)}, /*index=5*/s32[]{:T(128)}, s32[]{:T(128)}) while((s32[]{:T(128)}, bf16[24,4096]{1,0:T(8,128)(2,1)S(1)}, bf16[24,2,96,2,96]{2,1,0,4,3:T(2,128)(2,1)S(1)}, ...), condition=%wide.region_4.5_spmd.clone, body=%wide.region_2.4_spmd.clone.sunk | while | flops 76771328 | bytes 1089621 | solution.py:89
  120.6 0.4 fusion.114
  122.2 0.4 fusion.114
  123.8 0.4 fusion.114
  125.4 0.4 fusion.114
  127.0 0.4 fusion.114
  128.6 0.4 fusion.114
  130.3 0.4 fusion.114
  131.9 0.4 fusion.114
  133.5 0.4 fusion.114
  135.1 0.4 fusion.114
  136.7 0.4 fusion.114
  138.3 0.4 fusion.114
  139.8 0.7 copy.54
  140.5 4.5 %all-to-all-start.1 = ((bf16[24,8,512]{2,0,1:T(8,128)(2,1)}), bf16[24,8,512]{2,0,1:T(8,128)(2,1)S(1)}, u32[]{:S(2)}, u32[]{:S(2)}) async-start(bf16[24,8,512]{2,0,1:T(8,128)(2,1)} %bitcast.89), calls=%async_computation.1 | async-start | bytes 393216 | tf_op jit(solution)/shard_map/all_to_all | solution.py:126
  145.1 8.2 %all-to-all-done.1 = bf16[24,8,512]{2,0,1:T(8,128)(2,1)S(1)} async-done(((bf16[24,8,512]{2,0,1:T(8,128)(2,1)}), bf16[24,8,512]{2,0,1:T(8,128)(2,1)S(1)}, u32[]{:S(2)}, u32[]{:S(2)}) %all-to-all-start.1) | async-done | bytes 196640 | tf_op jit(solution)/shard_map/all_to_all | solution.py:126
  153.6 0.8 copy.34
  (299 shorter events, 26.3 us)
Async XLA Ops:
  5.4 29.5 %all-to-all-start = ((bf16[8,24,512]{2,1,0:T(8,128)(2,1)}), bf16[8,24,512]{2,1,0:T(8,128)(2,1)S(1)}, u32[]{:S(2)}, u32[]{:S(2)}) async-start(bf16[8,24,512]{2,1,0:T(8,128)(2,1)} %all_to_all.26), calls=%async_computation | async-start | bytes 393216 | tf_op jit(solution)/shard_map/all_to_all | solution.py:122
  72.8 13.0 %slice-start = ((s8[4718592]{0:T(1024)(128)(4,1)}), s8[4194304]{0:T(1024)(128)(4,1)S(1)}, s32[]{:S(2)}) async-start(s8[4718592]{0:T(1024)(128)(4,1)} %bitcast.107), calls=%async_computation.2 | async-start | bytes 8388608
  74.4 11.5 %slice-start.1 = ((s8[4718592]{0:T(1024)(128)(4,1)}), s8[524288]{0:T(1024)(128)(4,1)S(1)}, s32[]{:S(2)}) async-start(s8[4718592]{0:T(1024)(128)(4,1)} %bitcast.107), calls=%async_computation.3 | async-start | bytes 1048576
  140.5 12.8 %all-to-all-start.1 = ((bf16[24,8,512]{2,0,1:T(8,128)(2,1)}), bf16[24,8,512]{2,0,1:T(8,128)(2,1)S(1)}, u32[]{:S(2)}, u32[]{:S(2)}) async-start(bf16[24,8,512]{2,0,1:T(8,128)(2,1)} %bitcast.89), calls=%async_computation.1 | async-start | bytes 393216 | tf_op jit(solution)/shard_map/all_to_all | solution.py:126
